TPU v7x, 32 devices: a whole 2x2x4 slice. The times are simulated.
32 devices in a mesh: gx: 8 (over z, y), gy: 4 (over x, core).
Axes of the slice: x: 2, y: 2, z: 4, core: 2. Of those that a mesh axis runs over, the one named last changes fastest.
Arguments:
- states: bfloat16 [80, 8, 256, 1024], P('gx', None, 'gy'), may hold values from -6 to 6
- obs_pert: bfloat16 [80, 4, 1024], P(None, 'gy', 'gx'), may hold values from -6 to 6
- obs_innov: bfloat16 [4, 1024], P('gy', 'gx'), may hold values from -6 to 6
- obs_cell: int32 [4, 1024], P('gy', 'gx'), may hold values from 0 to 8191
- obs_count: int32 [4, 8], P('gy', 'gx'), may hold values from 16 to 128, as said below
Outputs:
- analysis: bfloat16 [80, 8, 256, 1024], P(None, None, 'gy', 'gx')
Inputs may be any that keep to these rules, and one draw needn't show every extreme that they name: `obs_count`: at most 128; some tile has exactly 128. `obs_cell`: slots at or after their tile's count are unused.
All inputs are finite; a program needn't handle non-finite values.
Results may differ from a plain program's by a relative error of at most 0.0057.
Values may be sent and summed in bfloat16 or wider, within the bound.
A program may use at most 128 MiB of HBM per device.

v0:
```python
import jax
import jax.numpy as jnp
from jax import lax
from jax.sharding import PartitionSpec as P

TX = 128
TY = 64
NS_ITERS = 4


def padded(cells, sides, width, closed):
    for axis, dim in sides:
        count = lax.axis_size(axis)
        ends = count if closed else count - 1
        head = lax.slice_in_dim(cells, 0, width, axis=dim)
        tail = lax.slice_in_dim(cells, cells.shape[dim] - width, cells.shape[dim], axis=dim)
        cells = jnp.concatenate(
            [
                lax.ppermute(tail, axis, [(i, (i + 1) % count) for i in range(ends)]),
                cells,
                lax.ppermute(head, axis, [((i + 1) % count, i) for i in range(ends)]),
            ],
            axis=dim,
        )
    return cells


def from_partner(value, axis, bit):
    mask = 2**bit
    pairs = [(source, source ^ mask) for source in range(lax.axis_size(axis))]
    return lax.ppermute(value, axis, pairs)


def locality(groups, row_index, col_index, tile_rows, tile_cols):
    slot_count = groups.shape[1] // 9
    width_x = TX * tile_cols
    height_y = TY * tile_rows
    position = lax.broadcasted_iota(jnp.int32, (1, 9 * slot_count), 1)
    row_shift = position // (3 * slot_count) - 1
    col_shift = position // slot_count % 3 - 1
    folded = jnp.logical_and(row_index == tile_rows - 1, row_shift == 1)
    src_row = jnp.where(folded, tile_rows - 1, row_index + row_shift)
    src_col = jnp.where(
        folded,
        (tile_cols - 1 - col_index + col_shift) % tile_cols,
        (col_index + col_shift) % tile_cols,
    )
    local_row = groups[-2:-1].astype(jnp.float32)
    local_col = groups[-1:].astype(jnp.float32)
    obs_y = src_row.astype(jnp.float32) * TY + local_row
    obs_x = src_col.astype(jnp.float32) * TX + local_col
    obs_y = jnp.where(folded, 2.0 * height_y - 1.0 - obs_y, obs_y)
    obs_x = jnp.where(folded, width_x - 1.0 - obs_x, obs_x)
    block_y = (row_index * TY + lax.broadcasted_iota(jnp.int32, (TY, 1), 0)).astype(jnp.float32)
    gap_y = obs_y - block_y
    offset = jnp.mod(obs_x - (col_index * TX).astype(jnp.float32), float(width_x))
    gap_x = jnp.where(offset < TX, 0.0, jnp.minimum(offset - (TX - 1.0), width_x - offset))
    radius = float(TY // 2)
    scaled = jnp.minimum(1.0, (gap_x * gap_x + gap_y * gap_y) / (radius * radius))
    return (1.0 - scaled) * (1.0 - scaled)


def batched(left, right):
    return jnp.einsum("bij,bjk->bik", left, right, precision=lax.Precision.HIGHEST)


def transforms(groups, taper, members):
    rows = groups[: members + 1]
    weighted = (rows.astype(jnp.float32)[None] * taper[:, None, :]).astype(jnp.bfloat16)
    products = jnp.einsum(
        "bks,js->bkj", weighted, groups[:members], preferred_element_type=jnp.float32
    )
    covariance = products[:, :members, :]
    projected = products[:, members, :]
    identity = jnp.eye(members, dtype=jnp.float32)
    system = identity[None] + covariance / (members - 1.0)
    norm_scale = jnp.sqrt(jnp.sum(system * system, axis=(1, 2)))[:, None, None]
    iterate = system / norm_scale
    inverse = jnp.broadcast_to(identity, system.shape)
    for sweep in range(NS_ITERS):
        correction = 1.5 * identity[None] - 0.5 * batched(inverse, iterate)
        iterate = batched(iterate, correction)
        inverse = batched(correction, inverse)
    spread_weights = inverse / jnp.sqrt(norm_scale)
    mean_weights = batched(inverse, batched(inverse, projected[:, :, None])) / (
        norm_scale * (members - 1.0)
    )
    return (spread_weights + mean_weights).astype(jnp.bfloat16)


def analysis_step(tile_states, transform):
    average = jnp.mean(tile_states.astype(jnp.float32), axis=0)
    perturb = (tile_states.astype(jnp.float32) - average[None]).astype(jnp.bfloat16)
    mixed_members = jnp.einsum(
        "klrx,rkj->jlrx", perturb, transform, preferred_element_type=jnp.float32
    )
    return (average[None] + mixed_members).astype(jnp.bfloat16)


def body(states, obs_pert, obs_innov, obs_cell, obs_count):
    members = obs_pert.shape[0]
    slot_count = obs_pert.shape[2]
    tile_cols = lax.axis_size("gx")
    tile_rows = lax.axis_size("gy")
    col_index = lax.axis_index("gx")
    row_index = lax.axis_index("gy")
    filled = lax.broadcasted_iota(jnp.int32, (1, slot_count), 1) < obs_count
    perturbs = obs_pert[:, 0, :]
    perturbs = jnp.where(filled, perturbs, jnp.zeros_like(perturbs))
    innovation = jnp.where(filled, obs_innov, jnp.zeros_like(obs_innov))
    packed = jnp.concatenate(
        [
            perturbs,
            innovation,
            (obs_cell // TX).astype(jnp.bfloat16),
            (obs_cell % TX).astype(jnp.bfloat16),
        ],
        axis=0,
    )
    extended = padded(packed, (("gx", 1),), slot_count, True)
    stacked = padded(extended[:, None, :], (("gy", 1),), 1, False)
    bit_total = tile_cols.bit_length() - 1
    mirror = extended
    for bit_number in range(bit_total):
        mirror = from_partner(mirror, "gx", bit_number)
    at_north = row_index == tile_rows - 1
    northern = jnp.where(at_north, mirror, stacked[:, 2, :])
    groups = jnp.concatenate([stacked[:, 0, :], stacked[:, 1, :], northern], axis=1)
    taper = locality(groups, row_index, col_index, tile_rows, tile_cols)
    transform = transforms(groups, taper, members)
    return analysis_step(
        lax.all_to_all(states, "gx", split_axis=3, concat_axis=0, tiled=True), transform
    )


def solution(mesh):
    return jax.shard_map(
        body,
        mesh=mesh,
        in_specs=(
            P("gx", None, "gy", None),
            P(None, "gy", "gx"),
            P("gy", "gx"),
            P("gy", "gx"),
            P("gy", "gx"),
        ),
        out_specs=P(None, None, "gy", "gx"),
        check_vma=False,
    )
```

profile of v0, /device:TPU:13, one launch (start us, length us, event | category | flops | bytes accessed | tf_op | source)
XLA Modules:
  0.0 479.4 jit_solution(11164224554101550364)
XLA Ops:
  0.0 25.1 %copy.65 = bf16[10,8,64,1024]{2,1,0,3:T(8,128)(2,1)} copy(bf16[10,8,64,1024]{3,2,1,0:T(8,128)(2,1)} %param.5) | data formatting | bytes 20971520 | tf_op args[0]
  25.1 19.7 %reshape.365 = bf16[8,2,327680]{2,1,0:T(2,128)(2,1)} reshape(bf16[1024,10,8,64]{3,2,1,0:T(8,128)(2,1)} %bitcast.63) | data formatting | bytes 20971520
  44.8 5.8 %all-to-all-start = ((bf16[8,2,327680]{2,1,0:T(2,128)(2,1)}), bf16[8,2,327680]{2,1,0:T(2,128)(2,1)}, u32[]{:S(2)}, u32[]{:S(2)}) async-start(bf16[8,2,327680]{2,1,0:T(2,128)(2,1)} %reshape.365), calls=%async_computation | async-start | bytes 20971520 | tf_op jit(solution)/shard_map/all_to_all | solution.py:132
  51.3 0.0 copy-done.2
  51.4 0.3 collective-permute-start.1
  51.7 2.1 collective-permute-start
  53.9 0.1 copy.68
  53.9 222.9 %collective-permute-done.1 = bf16[83,128]{1,0:T(8,128)(2,1)S(1)} collective-permute-done((bf16[83,128]{1,0:T(8,128)(2,1)S(1)}, bf16[83,128]{1,0:T(8,128)(2,1)S(1)}, u32[]{:S(2)}, u32[]{:S(2)}) %collective-permute-start.1) | collective-permute-done | bytes 21280 | tf_op jit(solution)/shard_map/ppermute | solution.py:21
  276.8 0.0 collective-permute-done
  276.9 5.1 %collective-permute-start.2 = (bf16[83,1,384]{2,0,1:T(8,128)(2,1)S(1)}, bf16[83,1,384]{2,0,1:T(8,128)(2,1)S(1)}, u32[]{:S(2)}, u32[]{:S(2)}) collective-permute-start(bf16[83,1,384]{2,0,1:T(8,128)(2,1)S(1)} %fusion.85), channel_id=1, source_target_pairs={{0,1},{1,2},{2,3},{4,5},{5,6},{6,7},{8,9},{9,10},{10,11},{12,13},{... | collective-permute-start | bytes 191240 | tf_op jit(solution)/shard_map/ppermute | solution.py:19
  282.0 0.1 collective-permute-start.3
  282.1 2.1 collective-permute-start.6
  284.2 1.0 collective-permute-done.3
  285.2 0.0 collective-permute-start.4
  285.2 0.0 collective-permute-done.2
  285.2 3.9 collective-permute-done.4
  289.1 0.0 collective-permute-start.5
  289.1 0.0 collective-permute-done.6
  289.1 4.0 collective-permute-done.5
  293.2 0.1 fusion.54
  293.3 0.1 subtract_multiply_fusion
  293.5 5.7 %fusion.2 = f32[64,81,80]{1,2,0:T(8,128)S(1)} fusion(f32[64,1152]{1,0:T(8,128)S(1)} %subtract_multiply_fusion, f32[81,1152]{1,0:T(8,128)S(1)} %slice_convert_fusion, bf16[83,1152]{1,0:T(8,128)(2,1)S(1)} %fusion.40), kind=kOutput, calls=%fused_computation.5 | convolution fusion | flops 967458816 | bytes 2543616 | tf_op jit(solution)/shard_map/bks,js->bkj/dot_general | solution.py:70
  299.3 1.9 slice_reduce_fusion
  301.1 0.7 multiply_reduce_fusion
  301.8 4.7 fusion.31
  306.5 4.5 fusion.15
  310.9 4.7 fusion.14
  315.6 2.8 fusion.66
  318.4 3.4 fusion.17
  321.8 3.0 fusion.16
  324.8 2.8 fusion.67
  327.6 3.2 fusion.19
  330.8 3.1 fusion.18
  334.0 3.1 fusion.68
  337.1 3.0 fusion.11
  340.2 4.2 convolution_bitcast_fusion
  344.3 4.6 fusion.69
  348.9 0.1 broadcast_divide_fusion
  349.0 0.0 all-to-all-done
  349.0 19.5 %reshape.366 = bf16[1024,10,8,64]{3,2,1,0:T(8,128)(2,1)} reshape(bf16[8,2,327680]{2,1,0:T(2,128)(2,1)} %all-to-all-done) | data formatting | bytes 20971520
  368.5 16.3 %convert_reduce_fusion = f32[8,64,1024]{1,0,2:T(8,128)} fusion(bf16[1024,10,8,64]{3,2,1,0:T(8,128)(2,1)} %reshape.366), kind=kLoop, calls=%fused_computation.10 | loop fusion | flops 9961472 | bytes 12582912 | tf_op jit(solution)/shard_map/reduce_sum | solution.py:92
  384.8 14.5 %bitcast_convert_fusion = f32[10,8,64,1024]{2,1,0,3:T(8,128)} fusion(bf16[1024,10,8,64]{3,2,1,0:T(8,128)(2,1)S(1)} %copy-done), kind=kLoop, calls=%fused_computation.118 | loop fusion | flops 5242880 | bytes 31457280 | tf_op jit(solution)/shard_map/convert_element_type | solution.py:92
  399.2 2.5 reduce_sum.27
  401.7 0.2 copy.66
  402.0 0.2 copy.67
  402.2 32.1 %copy.74 = f32[8,10,8,64,128]{4,3,2,1,0:T(8,128)} copy(f32[8,10,8,64,128]{3,2,1,4,0:T(8,128)} %bitcast.62) | data formatting | bytes 41943040 | tf_op jit(solution)/shard_map/convert_element_type | solution.py:92
  434.3 30.1 %fusion = bf16[80,8,64,128]{3,0,1,2:T(8,128)(2,1)} fusion(f32[8,64,128]{2,0,1:T(8,128)S(1)} %copy.67, f32[80,8,64,128]{3,2,1,0:T(8,128)} %bitcast.61, f32[64,80,80]{2,1,0:T(8,128)S(1)} %fusion.11, f32[64,80]{1,0:T(8,128)S(1)} %broadcast_divide_fusion, f32[64]{0:T(128)S(1)} %get-tuple-element.7), kind=kOutput, calls=%fused_computation.2 | convolution fusion | flops 861061120 | bytes 33378560 | tf_op jit(solution)/shard_map/klrx,rkj->jlrx/dot_general | solution.py:94
  464.4 14.8 %copy.77 = bf16[80,8,64,128]{3,2,1,0:T(8,128)(2,1)} copy(bf16[80,8,64,128]{3,0,1,2:T(8,128)(2,1)} %fusion) | data formatting | bytes 20971520 | tf_op jit(solution)/shard_map/convert_element_type | solution.py:97
  (25 shorter events, 0.3 us)
Async XLA Ops:
  44.8 6.5 %copy-start.2 = (bf16[1,128]{1,0:T(2,128)(2,1)S(1)}, bf16[1,128]{1,0:T(2,128)(2,1)}, u32[]{:S(2)}) copy-start(bf16[1,128]{1,0:T(2,128)(2,1)} %param.7) | copy-start | bytes 772
  44.8 6.5 %copy-start.3 = (s32[1,128]{1,0:T(1,128)S(1)}, s32[1,128]{1,0:T(1,128)}, u32[]{:S(2)}) copy-start(s32[1,128]{1,0:T(1,128)} %param.8) | copy-start | bytes 1540
  44.8 6.5 %copy-start.1 = (bf16[80,1,128]{2,0,1:T(8,128)(2,1)S(1)}, bf16[80,1,128]{2,0,1:T(8,128)(2,1)}, u32[]{:S(2)}) copy-start(bf16[80,1,128]{2,0,1:T(8,128)(2,1)} %param.6) | copy-start | bytes 61444
  44.8 304.2 %all-to-all-start = ((bf16[8,2,327680]{2,1,0:T(2,128)(2,1)}), bf16[8,2,327680]{2,1,0:T(2,128)(2,1)}, u32[]{:S(2)}, u32[]{:S(2)}) async-start(bf16[8,2,327680]{2,1,0:T(2,128)(2,1)} %reshape.365), calls=%async_computation | async-start | bytes 20971520 | tf_op jit(solution)/shard_map/all_to_all | solution.py:132
  51.4 225.4 %collective-permute-start.1 = (bf16[83,128]{1,0:T(8,128)(2,1)S(1)}, bf16[83,128]{1,0:T(8,128)(2,1)S(1)}, u32[]{:S(2)}, u32[]{:S(2)}) collective-permute-start(bf16[83,128]{1,0:T(8,128)(2,1)S(1)} %pad_maximum_fusion.1), channel_id=1, source_target_pairs={{4,0},{8,4},{12,8},{16,12},{20,16},{24,20},{28,24},{0,28},{5,1},{9... | collective-permute-start | bytes 63752 | tf_op jit(solution)/shard_map/ppermute | solution.py:21
  51.7 225.1 %collective-permute-start = (bf16[83,128]{1,0:T(8,128)(2,1)S(1)}, bf16[83,128]{1,0:T(8,128)(2,1)S(1)}, u32[]{:S(2)}, u32[]{:S(2)}) collective-permute-start(bf16[83,128]{1,0:T(8,128)(2,1)S(1)} %pad_maximum_fusion.1), channel_id=1, source_target_pairs={{0,4},{4,8},{8,12},{12,16},{16,20},{20,24},{24,28},{28,0},{1,5},{5... | collective-permute-start | bytes 63752 | tf_op jit(solution)/shard_map/ppermute | solution.py:19
  276.9 8.3 %collective-permute-start.2 = (bf16[83,1,384]{2,0,1:T(8,128)(2,1)S(1)}, bf16[83,1,384]{2,0,1:T(8,128)(2,1)S(1)}, u32[]{:S(2)}, u32[]{:S(2)}) collective-permute-start(bf16[83,1,384]{2,0,1:T(8,128)(2,1)S(1)} %fusion.85), channel_id=1, source_target_pairs={{0,1},{1,2},{2,3},{4,5},{5,6},{6,7},{8,9},{9,10},{10,11},{12,13},{... | collective-permute-start | bytes 191240 | tf_op jit(solution)/shard_map/ppermute | solution.py:19
  282.0 3.2 collective-permute-start.3
  282.1 7.1 %collective-permute-start.6 = (bf16[83,1,384]{2,0,1:T(8,128)(2,1)S(1)}, bf16[83,1,384]{2,0,1:T(8,128)(2,1)S(1)}, u32[]{:S(2)}, u32[]{:S(2)}) collective-permute-start(bf16[83,1,384]{2,0,1:T(8,128)(2,1)S(1)} %fusion.85), channel_id=1, source_target_pairs={{1,0},{2,1},{3,2},{5,4},{6,5},{7,6},{9,8},{10,9},{11,10},{13,12},{... | collective-permute-start | bytes 191240 | tf_op jit(solution)/shard_map/ppermute | solution.py:21
  285.2 4.0 collective-permute-start.4
  289.1 4.0 collective-permute-start.5
  368.5 16.3 %copy-start = (bf16[1024,10,8,64]{3,2,1,0:T(8,128)(2,1)S(1)}, bf16[1024,10,8,64]{3,2,1,0:T(8,128)(2,1)}, u32[]{:S(2)}) copy-start(bf16[1024,10,8,64]{3,2,1,0:T(8,128)(2,1)} %reshape.366) | copy-start | bytes 31457284
where the time goes:
time: 488 us; the launch traced here: 479 us
  waiting for transfers between devices  232 us (48%)
  local copies, waits for them, and re-layouts  114 us (23%)
  matrix products  82.8 us (17%)
  other arithmetic  34.6 us (7%)
  starting transfers between devices  15.5 us (3%)
    ppermute x2, waiting for transfers between devices, padded(): lax.ppermute(head, axis, [((i + 1) % count, i) for i in range(ends)])  223 us
    unnamed x14, local copies, waits for them, and re-layouts  64.3 us
    dot_general x13, matrix products, batched(): jnp.einsum('bij,bjk->bik', left, right, precision=lax.Precision.HIGHEST)  47 us
    convert_element_type x1, local copies, waits for them, and re-layouts, analysis_step(): average = jnp.mean(tile_states.astype(jnp.float32), axis=0)  32.1 us
    dot_general x1, matrix products, analysis_step(): jnp.einsum('klrx,rkj->jlrx', perturb, transform, preferred_element_type=j...  30.1 us
    reduce_sum x2, other arithmetic, analysis_step(): average = jnp.mean(tile_states.astype(jnp.float32), axis=0)  18.8 us
    convert_element_type x1, local copies, waits for them, and re-layouts, analysis_step(): return (average[None] + mixed_members).astype(jnp.bfloat16)  14.8 us
    convert_element_type x1, other arithmetic, analysis_step(): average = jnp.mean(tile_states.astype(jnp.float32), axis=0)  14.5 us
  transfers between devices with their start and end apart: 8, of which 4 were waited for; matrix products, arithmetic and copies ran while one was open for 12% of the time, Pallas kernels for 0%

commit v1 on v0

v1 whole, which is shorter than its diff:
```python
import functools

import jax
import jax.numpy as jnp
from jax import lax
from jax.experimental import pallas as pl
from jax.experimental.pallas import tpu as pltpu
from jax.sharding import PartitionSpec as P

TX = 128
TY = 64
NS_ITERS = 4
GROUP = 8
PACK = 96
PIECES = 8
MESH = pl.DeviceIdType.MESH


def split(value):
    high = value.astype(jnp.bfloat16)
    low = (value - high.astype(jnp.float32)).astype(jnp.bfloat16)
    return high, low


def product(left, right):
    dims = (((2,), (1,)), ((0,), (0,)))

    def one(a, b):
        return lax.dot_general(a, b, dims, preferred_element_type=jnp.float32)

    return one(left[0], right[0]) + (one(left[0], right[1]) + one(left[1], right[0]))


def emit(source, out):
    out[...] = source[...]


def pack(members, perturbs, innovation, cells, count, out):
    slot_count = out.shape[1]
    spot = lax.broadcasted_iota(jnp.int32, (members, slot_count), 1)
    live = perturbs[...].astype(jnp.float32)
    out[0:members, :] = jnp.where(spot < count[0, 0], live, 0.0).astype(jnp.bfloat16)
    rest = PACK - members
    spot = lax.broadcasted_iota(jnp.int32, (rest, slot_count), 1)
    level = lax.broadcasted_iota(jnp.int32, (rest, slot_count), 0)
    fresh = jnp.where(spot < count[0, 0], innovation[...].astype(jnp.float32), 0.0)
    place = cells[...]
    rows = (place // TX).astype(jnp.float32)
    columns = (place % TX).astype(jnp.float32)
    tail = jnp.where(level == 1, rows, jnp.where(level == 2, columns, 0.0))
    out[members:PACK, :] = jnp.where(level == 0, fresh, tail).astype(jnp.bfloat16)


def kernel(
    members, tile_cols, tile_rows,
    states, packed, out,
    held, groups, geometry, weights, spread, mixed, average, staged,
    send_sem, recv_sem, obs_send, obs_recv, fold_send, out_sem,
):
    col = lax.axis_index("gx")
    row = lax.axis_index("gy")
    per = members // tile_cols
    levels = states.shape[1]
    chunks = TY // GROUP

    barrier = pltpu.get_barrier_semaphore()

    def greet(step, carry):
        pl.semaphore_signal(
            barrier, inc=1, device_id=(lax.rem(col + step, tile_cols), row), device_id_type=MESH
        )
        return carry

    lax.fori_loop(1, tile_cols, greet, 0)
    for up in (1, tile_rows - 1):
        for side in (tile_cols - 1, 0, 1):
            pl.semaphore_signal(
                barrier, inc=1,
                device_id=(lax.rem(col + side, tile_cols), lax.rem(row + up, tile_rows)),
                device_id_type=MESH,
            )
    pl.semaphore_wait(barrier, tile_cols - 1 + 6)

    def slot(index):
        return groups.at[:, pl.ds(index * TX, TX)]

    def obs_copy(index, target_col, target_row, sems):
        return pltpu.make_async_remote_copy(
            src_ref=packed, dst_ref=slot(index), send_sem=sems, recv_sem=obs_recv.at[index],
            device_id=(target_col, target_row), device_id_type=MESH,
        )

    def obs_self(index):
        return pltpu.make_async_copy(packed, slot(index), obs_recv.at[index])

    def each_obs(act_remote, act_self):
        for side in (-1, 0, 1):
            target = lax.rem(col - side + tile_cols, tile_cols)
            first = 1 + side

            @pl.when(row < tile_rows - 1)
            def _():
                act_remote(obs_copy(first, target, row + 1, obs_send.at[first]))

            if side != 0:
                act_remote(obs_copy(3 + first, target, row, obs_send.at[3 + first]))

            @pl.when(row > 0)
            def _():
                act_remote(obs_copy(6 + first, target, row - 1, obs_send.at[6 + first]))

            folded = lax.rem(2 * tile_cols - 1 - col + side, tile_cols)

            @pl.when(jnp.logical_and(row == tile_rows - 1, folded != col))
            def _():
                act_remote(obs_copy(6 + first, folded, row, fold_send.at[first]))

            if act_self is not None:
                @pl.when(jnp.logical_and(row == tile_rows - 1, folded == col))
                def _():
                    act_self(obs_self(6 + first))

    each_obs(lambda copy: copy.start(), lambda copy: copy.start())
    obs_self(4).start()

    def state_copy(chunk, owner, target):
        return pltpu.make_async_remote_copy(
            src_ref=states.at[:, :, pl.ds(chunk * GROUP, GROUP), pl.ds(pl.multiple_of(target * TX, TX), TX)],
            dst_ref=held.at[chunk, pl.ds(owner * per, per)],
            send_sem=send_sem.at[chunk, target],
            recv_sem=recv_sem.at[chunk, owner],
            device_id=(target, row), device_id_type=MESH,
        )

    def own_copy(chunk):
        return pltpu.make_async_copy(
            states.at[:, :, pl.ds(chunk * GROUP, GROUP), pl.ds(pl.multiple_of(col * TX, TX), TX)],
            held.at[chunk, pl.ds(col * per, per)],
            recv_sem.at[chunk, col],
        )

    def launch(chunk, carry):
        def one(step, inner):
            state_copy(chunk, col, lax.rem(col + step, tile_cols)).start()
            return inner

        lax.fori_loop(1, tile_cols, one, 0)
        own_copy(chunk).start()
        return carry

    lax.fori_loop(0, chunks, launch, 0)

    obs_self(4).wait()
    for index in (3, 5):
        obs_copy(index, col, row, obs_send.at[index]).wait_recv()

    @pl.when(row > 0)
    def _():
        for index in range(3):
            obs_copy(index, col, row, obs_send.at[index]).wait_recv()

    @pl.when(row == 0)
    def _():
        groups[:, 0:3 * TX] = jnp.zeros((PACK, 3 * TX), jnp.bfloat16)

    for side in (-1, 0, 1):
        index = 7 + side
        folded = lax.rem(2 * tile_cols - 1 - col + side, tile_cols)
        alone = jnp.logical_and(row == tile_rows - 1, folded == col)

        @pl.when(alone)
        def _():
            obs_self(index).wait()

        @pl.when(jnp.logical_not(alone))
        def _():
            obs_copy(index, col, row, obs_send.at[index]).wait_recv()

    slots = 9 * TX
    width_x = TX * tile_cols
    height_y = TY * tile_rows
    position = lax.broadcasted_iota(jnp.int32, (1, slots), 1)
    row_shift = position // (3 * TX) - 1
    col_shift = position // TX % 3 - 1
    at_top = row == tile_rows - 1
    folded = jnp.logical_and(at_top, row_shift == 1)
    src_row = jnp.where(folded, tile_rows - 1, row + row_shift)
    src_col = jnp.where(
        folded,
        (2 * tile_cols - 1 - col + col_shift) % tile_cols,
        (col + col_shift + tile_cols) % tile_cols,
    )
    places = groups[members:PACK, :].astype(jnp.float32)
    local_row = places[1:2]
    local_col = places[2:3]
    obs_y = src_row.astype(jnp.float32) * TY + local_row
    obs_x = src_col.astype(jnp.float32) * TX + local_col
    obs_y = jnp.where(folded, 2.0 * height_y - 1.0 - obs_y, obs_y)
    obs_x = jnp.where(folded, width_x - 1.0 - obs_x, obs_x)
    away = obs_x - (col * TX).astype(jnp.float32)
    offset = jnp.where(away < 0.0, away + width_x, away)
    gap_x = jnp.where(offset < TX, 0.0, jnp.minimum(offset - (TX - 1.0), width_x - offset))
    geometry[0:1, :] = obs_y - (row * TY).astype(jnp.float32)
    geometry[1:2, :] = gap_x * gap_x

    radius = float(TY // 2)

    def transforms(step, carry):
        identity = (
            lax.broadcasted_iota(jnp.int32, (members, members), 0)
            == lax.broadcasted_iota(jnp.int32, (members, members), 1)
        ).astype(jnp.float32)
        systems = []
        projections = []
        scales = []
        for inner in range(GROUP):
            gap_y = geometry[0:1, :] - (step * GROUP + inner).astype(jnp.float32)
            scaled = jnp.minimum(1.0, (geometry[1:2, :] + gap_y * gap_y) / (radius * radius))
            taper = (1.0 - scaled) * (1.0 - scaled)
            weighted = (groups[...].astype(jnp.float32) * taper).astype(jnp.bfloat16)
            products = lax.dot_general(
                weighted, groups[0:members, :], (((1,), (1,)), ((), ())),
                preferred_element_type=jnp.float32,
            )
            system = identity + products[0:members] * (1.0 / (members - 1.0))
            square = jnp.sum(jnp.sum(system * system, axis=1, keepdims=True), axis=0, keepdims=True)
            systems.append(system)
            projections.append(products[members:members + 1])
            scales.append(jnp.sqrt(square))
        system = jnp.stack(systems)
        projected = jnp.stack(projections)
        norm_scale = jnp.stack(scales)
        iterate = system * (1.0 / norm_scale)
        inverse = None
        for sweep in range(NS_ITERS):
            iterate_parts = split(iterate)
            if inverse is None:
                correction = 1.5 * identity[None] - 0.5 * iterate
            else:
                inverse_parts = split(inverse)
                correction = 1.5 * identity[None] - 0.5 * product(inverse_parts, iterate_parts)
            correction_parts = split(correction)
            if sweep < NS_ITERS - 1:
                iterate = product(iterate_parts, correction_parts)
            inverse = correction if inverse is None else product(correction_parts, inverse_parts)
        half = jnp.sum(inverse * projected, axis=2, keepdims=True)
        mean = jnp.sum(inverse * half, axis=1, keepdims=True)
        mean = mean / (norm_scale * (members - 1.0))
        total = inverse * lax.rsqrt(norm_scale) + mean
        weights[pl.ds(step * GROUP, GROUP)] = total.astype(jnp.bfloat16)
        return carry

    lax.fori_loop(0, TY // GROUP, transforms, 0)

    def out_copy(chunk):
        return pltpu.make_async_copy(
            staged.at[lax.rem(chunk, 2)],
            out.at[:, :, pl.ds(chunk * GROUP, GROUP), :],
            out_sem.at[lax.rem(chunk, 2)],
        )

    def analyse(chunk, carry):
        def arrived(step, inner):
            owner = lax.rem(col + step, tile_cols)
            state_copy(chunk, owner, owner).wait_recv()
            return inner

        own_copy(chunk).wait()
        lax.fori_loop(1, tile_cols, arrived, 0)

        for level in range(levels):
            tile = held[chunk, :, level].astype(jnp.float32)
            mean = jnp.sum(tile, axis=0) * (1.0 / members)
            average[level] = mean
            perturb = (tile - mean[None]).astype(jnp.bfloat16).astype(jnp.float32)
            spread[level] = perturb.reshape(members * GROUP, TX)
        for inner in range(GROUP):
            block = jnp.concatenate(
                [
                    spread[level, pl.ds(inner, members, stride=GROUP), :].astype(jnp.bfloat16)
                    for level in range(levels)
                ],
                axis=1,
            )
            moved = jnp.dot(
                weights[chunk * GROUP + inner], block, preferred_element_type=jnp.float32
            )
            for level in range(levels):
                mixed[level, pl.ds(inner, members, stride=GROUP), :] = moved[:, level * TX:(level + 1) * TX]

        @pl.when(chunk >= 2)
        def _():
            out_copy(chunk - 2).wait()

        for level in range(levels):
            total = mixed[level].reshape(members, GROUP, TX) + average[level][None]
            staged[lax.rem(chunk, 2), :, level] = total.astype(jnp.bfloat16)
        out_copy(chunk).start()
        return carry

    lax.fori_loop(0, chunks, analyse, 0)
    out_copy(chunks - 2).wait()
    out_copy(chunks - 1).wait()

    def drain(chunk, carry):
        def one(step, inner):
            state_copy(chunk, col, lax.rem(col + step, tile_cols)).wait_send()
            return inner

        lax.fori_loop(1, tile_cols, one, 0)
        return carry

    lax.fori_loop(0, chunks, drain, 0)
    each_obs(lambda copy: copy.wait_send(), None)


def body(states, obs_pert, obs_innov, obs_cell, obs_count):
    members = obs_pert.shape[0]
    slot_count = obs_pert.shape[2]
    levels = states.shape[1]
    tile_cols = lax.axis_size("gx")
    tile_rows = lax.axis_size("gy")
    packed = pl.pallas_call(
        functools.partial(pack, members),
        out_shape=jax.ShapeDtypeStruct((PACK, slot_count), jnp.bfloat16),
        in_specs=[pl.BlockSpec(memory_space=pltpu.VMEM)] * 3 + [pl.BlockSpec(memory_space=pltpu.SMEM)],
        out_specs=pl.BlockSpec(memory_space=pltpu.VMEM),
    )(obs_pert.reshape(members, slot_count), obs_innov, obs_cell, obs_count)
    chunks = TY // GROUP
    result = pl.pallas_call(
        functools.partial(kernel, members, tile_cols, tile_rows),
        out_shape=jax.ShapeDtypeStruct((members, levels, TY, TX), jnp.bfloat16),
        in_specs=[pl.BlockSpec(memory_space=pltpu.HBM), pl.BlockSpec(memory_space=pltpu.VMEM)],
        out_specs=pl.BlockSpec(memory_space=pl.ANY),
        scratch_shapes=[
            pltpu.VMEM((chunks, members, levels, GROUP, TX), jnp.bfloat16),
            pltpu.VMEM((PACK, 9 * slot_count), jnp.bfloat16),
            pltpu.VMEM((8, 9 * slot_count), jnp.float32),
            pltpu.VMEM((TY, members, members), jnp.bfloat16),
            pltpu.VMEM((levels, members * GROUP, TX), jnp.float32),
            pltpu.VMEM((levels, members * GROUP, TX), jnp.float32),
            pltpu.VMEM((levels, GROUP, TX), jnp.float32),
            pltpu.VMEM((2, members, levels, GROUP, TX), jnp.bfloat16),
            pltpu.SemaphoreType.DMA((chunks, tile_cols)),
            pltpu.SemaphoreType.DMA((chunks, tile_cols)),
            pltpu.SemaphoreType.DMA((9,)),
            pltpu.SemaphoreType.DMA((9,)),
            pltpu.SemaphoreType.DMA((3,)),
            pltpu.SemaphoreType.DMA((2,)),
        ],
        compiler_params=pltpu.CompilerParams(
            collective_id=0, has_side_effects=True, vmem_limit_bytes=56 * 1024 * 1024
        ),
    )(states, packed)
    step = members // PIECES
    block = pl.BlockSpec((step, levels, TY, TX), lambda piece: (piece, 0, 0, 0))
    return pl.pallas_call(
        emit,
        grid=(PIECES,),
        out_shape=jax.ShapeDtypeStruct(result.shape, result.dtype),
        in_specs=[block],
        out_specs=block,
    )(result)


def solution(mesh):
    return jax.shard_map(
        body,
        mesh=mesh,
        in_specs=(
            P("gx", None, "gy", None),
            P(None, "gy", "gx"),
            P("gy", "gx"),
            P("gy", "gx"),
            P("gy", "gx"),
        ),
        out_specs=P(None, None, "gy", "gx"),
        check_vma=False,
    )
```

time: 488 us -> 251 us (0.51); the launches traced: 479 us -> 250 us
  Pallas kernels: 0 us -> 250 us
  waiting for transfers between devices: 232 us -> 0 us
  local copies, waits for them, and re-layouts: 114 us -> 0 us
  matrix products: 82.8 us -> 0 us
  other arithmetic: 34.6 us -> 0 us
  starting transfers between devices: 15.5 us -> 0 us
    pallas_call x0 -> x3, Pallas kernels: none -> 250 us  [the longest x1 238 us: body(): pl.pallas_call(functools.partial(kernel, members, tile_cols, tile_rows),...]
    ppermute x7 -> x0, waiting for transfers between devices: 232 us -> none  [the longest x2 223 us: padded(): lax.ppermute(head, axis, [((i + 1) % count, i) for i in range(ends)])]
    dot_general x15 -> x0, matrix products: 82.8 us -> none  [the longest x13 47 us: batched(): jnp.einsum('bij,bjk->bik', left, right, precision=lax.Precision.HIGHEST)]
    unnamed x14 -> x0, local copies, waits for them, and re-layouts: 64.3 us -> none
    convert_element_type x2 -> x0, local copies, waits for them, and re-layouts: 46.9 us -> none  [the longest x1 32.1 us: analysis_step(): average = jnp.mean(tile_states.astype(jnp.float32), axis=0)]
    reduce_sum x3 -> x0, other arithmetic: 19.5 us -> none  [the longest x2 18.8 us: analysis_step(): average = jnp.mean(tile_states.astype(jnp.float32), axis=0)]
    convert_element_type x5 -> x0, other arithmetic: 14.5 us -> none  [the longest x1 14.5 us: analysis_step(): average = jnp.mean(tile_states.astype(jnp.float32), axis=0)]
    ppermute x7 -> x0, starting transfers between devices: 9.65 us -> none  [the longest x2 7.15 us: padded(): lax.ppermute(tail, axis, [(i, (i + 1) % count) for i in range(ends)])]
  transfers between devices with their start and end apart: 8 -> 0, of which waited for: 4 -> 0; matrix products, arithmetic and copies ran while one was open for 12% -> 0% of each run, Pallas kernels for 0% -> 0%
where the time goes in v1:
time: 251 us; the launch traced here: 250 us
  Pallas kernels  250 us (100%)
    pallas_call x1, Pallas kernels, body(): pl.pallas_call(functools.partial(kernel, members, tile_cols, tile_rows),...  238 us
    pallas_call x1, Pallas kernels, body(): pl.pallas_call(emit, grid=(PIECES,), out_shape=jax.ShapeDtypeStruct(resul...  10.2 us

profile of v1, /device:TPU:13, one launch (start us, length us, event | category | flops | bytes accessed | tf_op | source)
XLA Modules:
  0.0 250.4 jit_solution(14531650642575503015)
XLA Ops:
  0.7 1.4 shard_map.55.packed
  2.0 238.2 %shard_map.56.source = bf16[80,8,64,128]{3,2,1,0:T(8,128)(2,1)} custom-call(bf16[10,8,64,1024]{3,2,1,0:T(8,128)(2,1)} %states.1, bf16[96,128]{1,0:T(8,128)(2,1)} %shard_map.55.packed), custom_call_target="tpu_custom_call" | custom-call | tf_op jit(solution)/shard_map/pallas_call | solution.py:330
  240.2 10.2 %shard_map.57 = bf16[80,8,64,128]{3,2,1,0:T(8,128)(2,1)} custom-call(bf16[80,8,64,128]{3,2,1,0:T(8,128)(2,1)} %shard_map.56.source), custom_call_target="tpu_custom_call" | custom-call | tf_op jit(solution)/shard_map/pallas_call | solution.py:357
